TPU v7x, 256 devices: a whole 4x4x8 slice. The times are simulated.
256 devices in a mesh: cluster: 8 (over x, core), leaf: 32 (over y, z).
Axes of the slice: x: 4, y: 4, z: 8, core: 2. Of those that a mesh axis runs over, the one named last changes fastest.
Arguments:
- probes: float32 [262144, 512], P(('cluster', 'leaf')), may hold values from -6 to 6
- dense_leaf: float32 [262144, 1024], P(('cluster', 'leaf')), may hold values from -0.1875 to 0.1875
- leaf_basis: float32 [262144, 128], P(('cluster', 'leaf')), may hold values from -0.1875 to 0.1875
- sibling_cores: float32 [256, 32, 128, 128], P(('cluster', 'leaf')), may hold values from -0.25 to 0.25
- transfer: float32 [256, 128, 128], P(('cluster', 'leaf')), may hold values from -0.5 to 0.5
- cluster_cores: float32 [8, 8, 128, 128], P('cluster'), may hold values from -0.0625 to 0.0625
Outputs:
- product: float32 [262144, 512], P(('cluster', 'leaf'))
All inputs are finite; a program needn't handle non-finite values.
Results may differ from a plain program's by a relative error of at most 0.00005.
Values sent between devices are 32-bit elements; how exact they have to be, the bound alone decides.
A program may use at most 128 MiB of HBM per device.

v0:
```python
import jax
import jax.numpy as jnp
from jax import lax
from jax.sharding import PartitionSpec as P

HI = lax.Precision.HIGHEST


def cut_along(array, dim, length):
    before, after = (array.shape[:dim], array.shape[dim + 1 :])
    return jnp.moveaxis(array.reshape(*before, length, -1, *after), dim, 0)


def summed_on_arrival(array, axis, dim):
    blocks = cut_along(array, dim, lax.axis_size(axis))
    arrived = lax.all_to_all(blocks, axis, split_axis=0, concat_axis=0, tiled=True)
    return arrived.sum(axis=0)


def joined_along(blocks, dim):
    blocks = jnp.moveaxis(blocks, 0, dim)
    lengths = blocks.shape
    return blocks.reshape(*lengths[:dim], lengths[dim] * lengths[dim + 1], *lengths[dim + 2 :])


def copy_for_each(array, axis):
    length = lax.axis_size(axis)
    return lax.all_to_all(
        jnp.broadcast_to(array[None], (length, *array.shape)), axis, 0, 0, tiled=True
    )


def gather_directly(array, axis, dim):
    return joined_along(copy_for_each(array, axis), dim)


def local(probes, dense_leaf, leaf_basis, sibling_cores, transfer, cluster_cores):
    own = lax.axis_index("leaf")
    cown = lax.axis_index("cluster")
    cores = sibling_cores[0]
    trans = transfer[0]
    outer_cores = cluster_cores[0]
    rank_two = trans.shape[1]
    near = jnp.dot(dense_leaf, probes, precision=HI) + jnp.dot(dense_leaf.T, probes, precision=HI)
    coef = jnp.dot(leaf_basis.T, probes, precision=HI)
    turned = lax.all_to_all(cores, "leaf", split_axis=0, concat_axis=0, tiled=True)
    used = cores + jnp.transpose(turned, (0, 2, 1))
    piece = lax.all_gather(coef[None], "leaf", axis=0, tiled=True)
    count = piece.shape[0]
    block = used
    keep = (jnp.arange(count, dtype=jnp.int32) != own).astype(jnp.float32)
    block = block * keep[:, None, None]
    sib = jnp.einsum("jab,jbp->ap", block, piece, precision=HI)
    local_g = jnp.dot(trans.T, coef, precision=HI)
    nclu = outer_cores.shape[0]
    bkeep = (jnp.arange(nclu, dtype=jnp.int32) != cown).astype(jnp.float32)[:, None, None]
    masked = outer_cores * bkeep
    g_piece = summed_on_arrival(local_g, "leaf", 1)
    gathered = gather_directly(g_piece[None], "cluster", 0)
    front = jnp.einsum("dab,dbp->ap", masked, gathered, precision=HI)
    number = rank_two * lax.axis_size("cluster") // rank_two
    block = masked
    terms = jnp.einsum("dba,bp->dap", block, g_piece, precision=HI)
    h_piece = front + summed_on_arrival(
        terms.reshape(number * rank_two, g_piece.shape[1]), "cluster", 0
    )
    field = gather_directly(h_piece, "leaf", 1)
    total = sib + jnp.dot(trans, field, precision=HI)
    return near + jnp.dot(leaf_basis, total, precision=HI)


def solution(mesh):
    return jax.shard_map(
        local,
        mesh=mesh,
        in_specs=(
            P(("cluster", "leaf"), None),
            P(("cluster", "leaf"), None),
            P(("cluster", "leaf"), None),
            P(("cluster", "leaf"), None, None, None),
            P(("cluster", "leaf"), None, None),
            P("cluster", None, None, None),
        ),
        out_specs=P(("cluster", "leaf"), None),
        check_vma=False,
    )
```

profile of v0, /device:TPU:4, one launch (start us, length us, event | category | flops | bytes accessed | tf_op | source)
XLA Modules:
  0.0 176.1 jit_solution(6064529818782093728)
XLA Ops:
  6.5 0.0 copy-start
  6.5 0.0 copy-start.4
  6.5 0.0 copy-start.2
  6.5 0.0 all-gather.3.cloned.1.call-start
  6.5 1.6 copy-done
  8.1 3.1 %fusion.20 = f32[128,512]{1,0:T(8,128)} fusion(f32[1024,128]{1,0:T(8,128)} %param.8, f32[1024,512]{1,0:T(8,128)S(1)} %copy-done), kind=kOutput, calls=%fused_computation.24 | convolution fusion | flops 805306368 | bytes 2883584 | tf_op jit(solution)/shard_map/dot_general | solution.py:45
  11.3 0.0 all-gather.3.cloned.1.call-update
  11.3 0.0 copy-done.4
  11.3 2.2 %fusion.14 = f32[512,128]{1,0:T(8,128)} fusion(f32[128,512]{1,0:T(8,128)} %fusion.20, f32[1,128,128]{2,1,0:T(8,128)S(1)} %copy-done.4), kind=kOutput, calls=%fused_computation.16 | convolution fusion | flops 100663296 | bytes 589824 | tf_op jit(solution)/shard_map/dot_general | solution.py:54
  13.5 11.5 %all-to-all-start.1 = ((f32[32,128,16]{1,2,0:T(8,128)}), f32[32,128,16]{1,2,0:T(8,128)S(1)}, u32[]{:S(2)}, u32[]{:S(2)}) async-start(f32[32,128,16]{1,2,0:T(8,128)} %bitcast.8), calls=%async_computation.1 | async-start | bytes 524288 | tf_op jit(solution)/shard_map/all_to_all | solution.py:16
  25.0 13.1 %all-to-all-done.1 = f32[32,128,16]{1,2,0:T(8,128)S(1)} async-done(((f32[32,128,16]{1,2,0:T(8,128)}), f32[32,128,16]{1,2,0:T(8,128)S(1)}, u32[]{:S(2)}, u32[]{:S(2)}) %all-to-all-start.1) | async-done | bytes 262176 | tf_op jit(solution)/shard_map/all_to_all | solution.py:16
  38.2 0.0 copy-done.2
  38.2 0.5 fusion.9
  38.7 7.7 %all_to_all.25 = f32[8,128,16]{1,2,0:T(8,128)S(1)} all-to-all(f32[8,128,16]{1,2,0:T(8,128)S(1)} %fusion.9), channel_id=1, replica_groups=mesh['cluster'=8,'leaf'=32] {'cluster'}, dimensions={0} | all-to-all | bytes 131072 | tf_op jit(solution)/shard_map/all_to_all | solution.py:16
  46.4 0.6 broadcast_in_dim.7
  47.0 5.8 %all-to-all-start.2 = ((f32[8,1,128,16]{2,3,1,0:T(8,128)}), f32[8,1,128,16]{2,3,1,0:T(8,128)S(1)}, u32[]{:S(2)}, u32[]{:S(2)}) async-start(f32[8,1,128,16]{2,3,1,0:T(8,128)} %broadcast_in_dim.7), calls=%async_computation.2 | async-start | bytes 131072 | tf_op jit(solution)/shard_map/all_to_all | solution.py:28
  52.8 2.9 %copy.12 = f32[32,128,128]{1,2,0:T(8,128)} copy(f32[32,128,128]{2,1,0:T(8,128)} %bitcast.60) | data formatting | bytes 4194304 | tf_op jit(solution)/shard_map/squeeze | solution.py:40
  55.7 0.2 all-to-all-done.2
  55.9 5.8 %all-to-all-start = ((f32[32,128,128]{1,2,0:T(8,128)}), f32[32,128,128]{1,2,0:T(8,128)}, u32[]{:S(2)}, u32[]{:S(2)}) async-start(f32[32,128,128]{1,2,0:T(8,128)} %copy.12), calls=%async_computation | async-start | bytes 4194304 | tf_op jit(solution)/shard_map/all_to_all | solution.py:46
  61.7 0.0 copy-start.1
  61.7 9.7 %fusion.19 = f32[1024,512]{1,0:T(8,128)} fusion(f32[1024,1024]{1,0:T(8,128)} %param.7, f32[1024,512]{1,0:T(8,128)S(1)} %copy-done), kind=kOutput, calls=%fused_computation.23 | convolution fusion | flops 6442450944 | bytes 8388608 | tf_op jit(solution)/shard_map/dot_general | solution.py:44
  71.5 0.0 copy-done.1
  71.5 8.0 %fusion.18 = f32[1024,512]{1,0:T(8,128)} fusion(f32[1024,1024]{1,0:T(8,128)S(1)} %copy-done.1, f32[1024,512]{1,0:T(8,128)S(1)} %copy-done), kind=kOutput, calls=%fused_computation.22 | convolution fusion | flops 6442450944 | bytes 8388608 | tf_op jit(solution)/shard_map/dot_general | solution.py:44
  79.5 0.6 fusion.7
  80.1 50.4 %all-to-all-done = f32[32,128,128]{1,2,0:T(8,128)} async-done(((f32[32,128,128]{1,2,0:T(8,128)}), f32[32,128,128]{1,2,0:T(8,128)}, u32[]{:S(2)}, u32[]{:S(2)}) %all-to-all-start) | async-done | bytes 2097184 | tf_op jit(solution)/shard_map/all_to_all | solution.py:46
  130.4 0.7 broadcast_in_dim.8
  131.1 9.7 %all-to-all-start.4 = ((f32[32,128,16]{1,2,0:T(8,128)}), f32[32,128,16]{1,2,0:T(8,128)S(1)}, u32[]{:S(2)}, u32[]{:S(2)}) async-start(f32[32,128,16]{1,2,0:T(8,128)} %broadcast_in_dim.8), calls=%async_computation.4 | async-start | bytes 524288 | tf_op jit(solution)/shard_map/all_to_all | solution.py:28
  140.8 14.7 %all-gather.3.cloned.1.call-done = f32[4096,512]{1,0:T(8,128)} async-done(((f32[128,512]{1,0:T(8,128)}), f32[4096,512]{1,0:T(8,128)}) %all-gather.3.cloned.1.call-update) | async-done | bytes 8388624 | tf_op jit(solution)/shard_map/all_gather | solution.py:48
  155.5 0.0 copy-start.3
  155.5 7.9 %fusion.3 = f32[128,512]{1,0:T(8,128)S(1)} fusion(f32[32,128,512]{2,1,0:T(8,128)} %bitcast.59, f32[32,128,128]{1,2,0:T(8,128)} %all-to-all-done, f32[32]{0:T(128)S(1)} %compare_convert_fusion.1, f32[1,32,128,128]{3,2,1,0:T(8,128)} %param.9), kind=kOutput, calls=%fused_computation.4 | convolution fusion | flops 3222274048 | bytes 12845184 | tf_op jit(solution)/shard_map/jab,jbp->ap/dot_general | solution.py:53
  163.4 0.0 all-to-all-done.4
  163.5 0.4 fusion.6
  163.8 0.0 copy-done.3
  163.9 5.4 %bitcast_add_fusion = f32[1024,512]{1,0:T(8,128)} fusion(f32[1024,512]{1,0:T(8,128)} %fusion.18, f32[1024,512]{1,0:T(8,128)} %fusion.19, f32[128,512]{1,0:T(8,128)S(1)} %fusion.6, f32[1024,128]{1,0:T(8,128)S(1)} %copy-done.3), kind=kOutput, calls=%fused_computation | convolution fusion | flops 806354944 | bytes 7077888 | tf_op jit(solution)/shard_map/dot_general | solution.py:69
  (4 shorter events, 0.1 us)
Async XLA Ops:
  6.5 1.6 copy-start
  6.5 4.7 %copy-start.4 = (f32[1,128,128]{2,1,0:T(8,128)S(1)}, f32[1,128,128]{2,1,0:T(8,128)}, u32[]{:S(2)}) copy-start(f32[1,128,128]{2,1,0:T(8,128)} %param.10) | copy-start | bytes 196612
  6.5 31.7 %copy-start.2 = (f32[1,8,128,128]{3,2,1,0:T(8,128)S(1)}, f32[1,8,128,128]{3,2,1,0:T(8,128)}, u32[]{:S(2)}) copy-start(f32[1,8,128,128]{3,2,1,0:T(8,128)} %param.11) | copy-start | bytes 1572868
  6.5 149.0 %all-gather.3.cloned.1.call-start = ((), (), s32[]{:S(2)}) async-start(), calls=%async_computation.5 | async-start | bytes 8650752 | tf_op jit(solution)/shard_map/all_gather | solution.py:48
  13.5 24.6 %all-to-all-start.1 = ((f32[32,128,16]{1,2,0:T(8,128)}), f32[32,128,16]{1,2,0:T(8,128)S(1)}, u32[]{:S(2)}, u32[]{:S(2)}) async-start(f32[32,128,16]{1,2,0:T(8,128)} %bitcast.8), calls=%async_computation.1 | async-start | bytes 524288 | tf_op jit(solution)/shard_map/all_to_all | solution.py:16
  47.0 8.9 %all-to-all-start.2 = ((f32[8,1,128,16]{2,3,1,0:T(8,128)}), f32[8,1,128,16]{2,3,1,0:T(8,128)S(1)}, u32[]{:S(2)}, u32[]{:S(2)}) async-start(f32[8,1,128,16]{2,3,1,0:T(8,128)} %broadcast_in_dim.7), calls=%async_computation.2 | async-start | bytes 131072 | tf_op jit(solution)/shard_map/all_to_all | solution.py:28
  55.9 74.5 %all-to-all-start = ((f32[32,128,128]{1,2,0:T(8,128)}), f32[32,128,128]{1,2,0:T(8,128)}, u32[]{:S(2)}, u32[]{:S(2)}) async-start(f32[32,128,128]{1,2,0:T(8,128)} %copy.12), calls=%async_computation | async-start | bytes 4194304 | tf_op jit(solution)/shard_map/all_to_all | solution.py:46
  61.7 9.7 %copy-start.1 = (f32[1024,1024]{1,0:T(8,128)S(1)}, f32[1024,1024]{1,0:T(8,128)}, u32[]{:S(2)}) copy-start(f32[1024,1024]{1,0:T(8,128)} %param.7) | copy-start | bytes 12582916
  131.1 32.3 %all-to-all-start.4 = ((f32[32,128,16]{1,2,0:T(8,128)}), f32[32,128,16]{1,2,0:T(8,128)S(1)}, u32[]{:S(2)}, u32[]{:S(2)}) async-start(f32[32,128,16]{1,2,0:T(8,128)} %broadcast_in_dim.8), calls=%async_computation.4 | async-start | bytes 524288 | tf_op jit(solution)/shard_map/all_to_all | solution.py:28
  155.5 8.3 %copy-start.3 = (f32[1024,128]{1,0:T(8,128)S(1)}, f32[1024,128]{1,0:T(8,128)}, u32[]{:S(2)}) copy-start(f32[1024,128]{1,0:T(8,128)} %param.8) | copy-start | bytes 1572868
Sparse Core Ops, SparseCore 0:
  11.4 144.0 all-gather.2
where the time goes:
time: 179 us; the launch traced here: 176 us
  waiting for transfers between devices  78.4 us (44%)
  matrix products  37.9 us (21%)
  starting transfers between devices  32.7 us (18%)
  between operations  13.5 us (8%)
  blocking collectives  7.69 us (4%)
  local copies, waits for them, and re-layouts  5.84 us (3%)
    all_to_all x1, waiting for transfers between devices, local(): lax.all_to_all(cores, 'leaf', split_axis=0, concat_axis=0, tiled=True)  50.4 us
    all_to_all x2, starting transfers between devices, copy_for_each(): lax.all_to_all(jnp.broadcast_to(array[None], (length, *array.shape)), axi...  15.5 us
    all_gather x1, waiting for transfers between devices, local(): piece = lax.all_gather(coef[None], 'leaf', axis=0, tiled=True)  14.7 us
    all_to_all x1, waiting for transfers between devices, summed_on_arrival(): lax.all_to_all(blocks, axis, split_axis=0, concat_axis=0, tiled=True)  13.1 us
    all_to_all x1, starting transfers between devices, summed_on_arrival(): lax.all_to_all(blocks, axis, split_axis=0, concat_axis=0, tiled=True)  11.5 us
    dot_general x1, matrix products, local(): jnp.dot(dense_leaf.T, probes, precision=HI)  9.71 us
    dot_general x1, matrix products, local(): jnp.dot(dense_leaf, probes, precision=HI)  8.01 us
    dot_general x1, matrix products, local(): sib = jnp.einsum('jab,jbp->ap', block, piece, precision=HI)  7.91 us
  transfers between devices with their start and end apart: 5, of which 4 were waited for; matrix products, arithmetic and copies ran while one was open for 19% of the time, Pallas kernels for 0%

commit v1 on v0

v1 whole, which is shorter than its diff:
```python
import jax
import jax.numpy as jnp
from jax import lax
from jax.experimental import pallas as pl
from jax.experimental.pallas import tpu as pltpu
from jax.sharding import PartitionSpec as P

MESH = pl.DeviceIdType.MESH
F32, BF16 = jnp.float32, jnp.bfloat16
NY, NZ, NC = 4, 8, 8
LEAF, R, PC = 1024, 128, 512
HALF = PC // 2
NN = (((1,), (0,)), ((), ()))
NT = (((1,), (1,)), ((), ()))


def split(v):
    hi = v.astype(BF16)
    return hi, (v - hi.astype(F32)).astype(BF16)


def dot3(a, b, dims):
    (ah, al), (bh, bl) = a, b

    def one(u, v):
        return lax.dot_general(u, v, dims, preferred_element_type=F32)

    return one(ah, bh) + one(ah, bl) + one(al, bh)


GROUPS = ((4,), (3, 5), (2, 6), (1, 7), (0,))
LENGTH = {(1, 0): 4, (1, 1): 3, (-1, 0): 3, (-1, 1): 4}
CHAINS = tuple(LENGTH)


def kernel(
    x_hbm, d_hbm, u_hbm, a_hbm, e_hbm, b_hbm, out_hbm,
    xv, dv, uv, xh, xl, a2, ah, al, cc, cr, crh, crl, er, bv, p2, rz, p1, ry, near, gs, gz, gp, gx, ts, tx, hp, hz, hy, tot,
    lsem, ssem, rsem,
):
    leaf = lax.axis_index("leaf")
    clu = lax.axis_index("cluster")
    y, z = leaf // NZ, lax.rem(leaf, NZ)
    counts = {"local": 0, "remote": 0}
    started = []

    def at_y(d):
        return {"leaf": lax.rem(y + d + NY, NY) * NZ + z}

    def at_z(d):
        return {"leaf": y * NZ + lax.rem(z + d + NZ, NZ)}

    def at_c(d):
        return {"cluster": lax.rem(clu + d + NC, NC)}

    barrier = pltpu.get_barrier_semaphore()
    partners = [at_y(d) for d in range(1, NY)] + [at_z(d) for d in range(1, NZ)] + [at_c(d) for d in range(1, NC)]
    for partner in partners:
        pl.semaphore_signal(barrier, inc=1, device_id=partner, device_id_type=MESH)

    def load(src, dst):
        i = counts["local"]
        counts["local"] += 1
        copy = pltpu.make_async_copy(src, dst, lsem.at[i])
        copy.start()
        return copy

    def send(src, dst, where):
        i = counts["remote"]
        counts["remote"] += 1
        copy = pltpu.make_async_remote_copy(
            src_ref=src, dst_ref=dst, send_sem=ssem.at[i], recv_sem=rsem.at[i], device_id=where, device_id_type=MESH
        )
        copy.start()
        started.append(copy)
        return copy

    load_x = load(x_hbm, xv)
    load_u = load(u_hbm, uv)
    load_d = load(d_hbm, dv)
    load_e = load(e_hbm.at[0], er.at[0])
    own_a = {d: load(a_hbm.at[0, y * NZ + lax.rem(z + d, NZ)], a2.at[0, d]) for d in range(1, NZ)}
    load_b = [load(b_hbm.at[0, lax.rem(clu - d + NC, NC)], bv.at[d]) for d in range(1, NC)]
    a2[0, 0] = jnp.zeros((R, R), F32)

    load_x.wait()
    load_u.wait()
    h, l = split(xv[...])
    xh[...] = h
    xl[...] = l
    coef = dot3(split(uv[...].T), (xh[...], xl[...]), NN).T
    cc[0] = coef
    cr[0] = coef

    pl.semaphore_wait(barrier, len(partners))

    def rows(half):
        return pl.ds(half * HALF, HALF)

    def slot(sign, step):
        return step if sign < 0 else (NZ - step) % NZ

    gather = {}

    def gather_step(chain, step):
        sign, half = chain
        gather[chain, step] = send(
            cc.at[slot(sign, step - 1), rows(half)], cc.at[slot(sign, step), rows(half)], at_z(sign)
        )

    for chain in CHAINS:
        gather_step(chain, 1)

    cores = {}

    def send_cores(d):
        for dy in (1, 3, 2):
            target = lax.rem(y + dy, NY) * NZ + lax.rem(z + d, NZ)
            cores[d, dy] = send(a_hbm.at[0, target], a2.at[NY - dy, d], at_y(dy))

    send_cores(4)
    rows_y = [send(cc.at[0], cr.at[NY - dy], at_y(dy)) for dy in (1, 3, 2)]
    maps_y = [send(e_hbm.at[0], er.at[NY - dy], at_y(dy)) for dy in (1, 3, 2)]
    for group in GROUPS[1:]:
        for d in group:
            send_cores(d)

    def relay(step):
        for chain in CHAINS:
            if step < LENGTH[chain]:
                gather[chain, step].wait_recv()
                gather_step(chain, step + 1)

    def near_chunk(i):
        size = LEAF // 4
        part = slice(i * size, (i + 1) * size)
        sym = dv[part, :] + dv[:, part].T
        near[part, :] = dot3(split(sym), (xh[...], xl[...]), NN)

    load_d.wait()
    near_chunk(0)
    relay(1)
    near_chunk(1)
    relay(2)
    near_chunk(2)

    for copy in rows_y + maps_y:
        copy.wait_recv()
    load_e.wait()
    mine = pl.ds(pl.multiple_of(y * R, R), R)
    g = jnp.zeros((R, R), F32)
    for r in range(NY):
        h, l = split(cr[r])
        crh[:, r * R : (r + 1) * R] = h
        crl[:, r * R : (r + 1) * R] = l
        g = g + dot3(split(cr[r, mine, :]), split(er[r]), NN)
    gs[...] = g
    PIECE = R // NZ

    def piece(at):
        return pl.ds(pl.multiple_of(at * PIECE, PIECE), PIECE)

    g_z = [send(gs.at[piece(lax.rem(z + d, NZ))], gz.at[d], at_z(d)) for d in range(1, NZ)]

    sums = {}

    def second(group):
        for d in group:
            for dy in (1, 3, 2):
                cores[d, dy].wait_recv()
            if d > 0:
                own_a[d].wait()
        for i, d in enumerate(group):
            h, l = split(a2[:, d].reshape(NY * R, R))
            ah[d] = h
            al[d] = l
        b = tuple(jnp.concatenate([m[d] for d in group], axis=1) for m in (ah, al))
        t = dot3((crh[...], crl[...]), b, NN)
        for i, d in enumerate(group):
            p2[d] = t[:, i * R : (i + 1) * R]

    def sum_step(chain, step):
        sign, half = chain
        left = LENGTH[chain] - step
        at = (sign * left) % NZ
        index = CHAINS.index(chain)
        if step > 0:
            sums[chain, step].wait_recv()
            p2[at, rows(half)] = p2[at, rows(half)] + rz[index, step - 1]
        sums[chain, step + 1] = send(p2.at[at, rows(half)], rz.at[index, step], at_z(sign))

    second(GROUPS[0])
    for chain in CHAINS:
        if LENGTH[chain] == 4:
            sum_step(chain, 0)
    second(GROUPS[1])
    for chain in CHAINS:
        if LENGTH[chain] == 3:
            sum_step(chain, 0)
    relay(3)

    for copy in g_z:
        copy.wait_recv()
    own_piece = gs[piece(z), :]
    for d in range(1, NZ):
        own_piece = own_piece + gz[d]
    gp[...] = own_piece
    g_c = [send(gp, gx.at[d], at_c(d)) for d in range(1, NC)]
    for copy in load_b:
        copy.wait()
    halves = split(own_piece)
    for d in range(1, NC):
        ts[d] = dot3(halves, split(bv[d]), NN)
    t_c = [send(ts.at[d], tx.at[d], at_c(-d)) for d in range(1, NC)]

    near_chunk(3)
    second(GROUPS[2])
    for chain in CHAINS:
        sum_step(chain, 1)

    for copy in g_c + t_c:
        copy.wait_recv()
    field = tx[1]
    for d in range(2, NC):
        field = field + tx[d]
    for d in range(1, NC):
        field = field + dot3(split(gx[d]), split(bv[d]), NT)
    hp[...] = field
    hz[piece(z), :] = field
    h_z = [send(hp, hz.at[piece(z)], at_z(d)) for d in range(1, NZ)]

    second(GROUPS[3])
    for chain in CHAINS:
        sum_step(chain, 2)

    for chain in CHAINS:
        gather[chain, LENGTH[chain]].wait_recv()

    def first(group, fresh):
        a = split(jnp.concatenate([cc[d] for d in group], axis=1))
        b = tuple(jnp.concatenate([m[d] for d in group], axis=1) for m in (ah, al))
        t = dot3(a, b, NT)
        for r in range(NY):
            new = t[:, r * R : (r + 1) * R]
            p1[r] = new if fresh else p1[r] + new

    first(GROUPS[0], True)
    first(GROUPS[1], False)

    for copy in h_z:
        copy.wait_recv()
    hy[mine, :] = hz[...]
    h_y = [send(hz, hy.at[mine], at_y(dy)) for dy in (1, 3, 2)]
    first(GROUPS[2], False)

    for chain in CHAINS:
        if LENGTH[chain] == 4:
            sum_step(chain, 3)
    first(GROUPS[3], False)
    second(GROUPS[4])
    first(GROUPS[4], False)
    sums_y = [send(p1.at[dy], ry.at[dy], at_y(dy)) for dy in (1, 3, 2)]

    total = p1[0] + p2[0]
    for copy in h_y:
        copy.wait_recv()
    total = total + dot3(split(hy[...]), split(er[0]), NT)
    tot[...] = total
    for chain in CHAINS:
        length = LENGTH[chain]
        sums[chain, length].wait_recv()
        half = rows(chain[1])
        tot[half, :] = tot[half, :] + rz[CHAINS.index(chain), length - 1]
    for copy in sums_y:
        copy.wait_recv()
    total = split(tot[...] + ry[1] + ry[2] + ry[3])
    writes = []
    for i in range(4):
        part = slice(i * 256, (i + 1) * 256)
        near[part, :] = near[part, :] + dot3(split(uv[part, :]), total, NT)
        writes.append(load(near.at[part], out_hbm.at[part]))
    for copy in started:
        copy.wait_send()
    for copy in writes:
        copy.wait()


N_LOCAL, N_REMOTE = 32, 112


def local(probes, dense_leaf, leaf_basis, sibling_cores, transfer, cluster_cores):
    hbm = pl.BlockSpec(memory_space=pl.ANY)
    vmem = pltpu.VMEM
    scratch = [
        vmem((LEAF, PC), F32), vmem((LEAF, LEAF), F32), vmem((LEAF, R), F32), vmem((LEAF, PC), BF16), vmem((LEAF, PC), BF16),
        vmem((NY, NZ, R, R), F32), vmem((NZ, NY * R, R), BF16), vmem((NZ, NY * R, R), BF16),
        vmem((NZ, PC, R), F32), vmem((NY, PC, R), F32), vmem((PC, NY * R), BF16), vmem((PC, NY * R), BF16),
        vmem((NY, R, R), F32), vmem((NC, R, R), F32),
        vmem((NZ, PC, R), F32), vmem((4, 4, HALF, R), F32), vmem((NY, PC, R), F32), vmem((NY, PC, R), F32), vmem((LEAF, PC), F32),
        vmem((R, R), F32), vmem((NZ, R // NZ, R), F32), vmem((R // NZ, R), F32), vmem((NC, R // NZ, R), F32),
        vmem((NC, R // NZ, R), F32), vmem((NC, R // NZ, R), F32), vmem((R // NZ, R), F32), vmem((R, R), F32), vmem((PC, R), F32),
        vmem((PC, R), F32),
        pltpu.SemaphoreType.DMA((N_LOCAL,)), pltpu.SemaphoreType.DMA((N_REMOTE,)), pltpu.SemaphoreType.DMA((N_REMOTE,)),
    ]
    return pl.pallas_call(
        kernel,
        out_shape=jax.ShapeDtypeStruct((LEAF, PC), F32),
        in_specs=[hbm] * 6,
        out_specs=hbm,
        scratch_shapes=scratch,
        compiler_params=pltpu.CompilerParams(collective_id=0, has_side_effects=True, vmem_limit_bytes=60 * 2**20),
    )(probes, dense_leaf, leaf_basis, sibling_cores, transfer, cluster_cores)


def solution(mesh):
    both = P(("cluster", "leaf"), None)
    return jax.shard_map(
        local,
        mesh=mesh,
        in_specs=(
            both, both, both, P(("cluster", "leaf"), None, None, None), P(("cluster", "leaf"), None, None),
            P("cluster", None, None, None),
        ),
        out_specs=both,
        check_vma=False,
    )
```

time: 179 us -> 74.8 us (0.42)
  waiting for transfers between devices: 78.4 us -> 0 us
  Pallas kernels: 0 us -> 70.6 us
  matrix products: 37.9 us -> 0 us
  starting transfers between devices: 32.7 us -> 0 us
  between operations: 13.5 us -> 0.01 us
  blocking collectives: 7.69 us -> 0 us
  local copies, waits for them, and re-layouts: 5.84 us -> 3.08 us
    pallas_call x0 -> x1, Pallas kernels: none -> 70.6 us  [local(): pl.pallas_call(kernel, out_shape=jax.ShapeDtypeStruct((LEAF, PC), F32), i...]
    all_to_all x4 -> x0, waiting for transfers between devices: 63.7 us -> none  [the longest x1 50.4 us: local(): lax.all_to_all(cores, 'leaf', split_axis=0, concat_axis=0, tiled=True)]
    dot_general x9 -> x0, matrix products: 37.9 us -> none  [the longest x1 9.71 us: local(): jnp.dot(dense_leaf.T, probes, precision=HI)]
    all_to_all x4 -> x0, starting transfers between devices: 32.7 us -> none  [the longest x2 15.5 us: copy_for_each(): lax.all_to_all(jnp.broadcast_to(array[None], (length, *array.shape)), axi...]
    all_gather x1 -> x0, waiting for transfers between devices: 14.7 us -> none  [local(): piece = lax.all_gather(coef[None], 'leaf', axis=0, tiled=True)]
    all_to_all x1 -> x0, blocking collectives: 7.69 us -> none  [summed_on_arrival(): lax.all_to_all(blocks, axis, split_axis=0, concat_axis=0, tiled=True)]
    squeeze x1 -> x0, local copies, waits for them, and re-layouts: 2.9 us -> none  [local(): cores = sibling_cores[0]]
  transfers between devices with their start and end apart: 5 -> 0, of which waited for: 4 -> 0; matrix products, arithmetic and copies ran while one was open for 19% -> 0% of each run, Pallas kernels for 0% -> 0%
where the time goes in v1:
time: 74.8 us; the launch traced here: 73.7 us
  Pallas kernels  70.6 us (94%)
  local copies, waits for them, and re-layouts  3.08 us (4%)
    pallas_call x1, Pallas kernels, local(): pl.pallas_call(kernel, out_shape=jax.ShapeDtypeStruct((LEAF, PC), F32), i...  70.6 us
    unnamed x1, local copies, waits for them, and re-layouts  3.08 us

profile of v1, /device:TPU:4, one launch (start us, length us, event | category | flops | bytes accessed | tf_op | source)
XLA Modules:
  0.0 73.7 jit_solution(18028901999664368722)
XLA Ops:
  0.0 70.6 %shard_map.64 = f32[1024,512]{1,0:T(8,128)} custom-call(f32[1024,512]{1,0:T(8,128)} %x_hbm.1, f32[1024,1024]{1,0:T(8,128)} %d_hbm.1, f32[1024,128]{1,0:T(8,128)} %u_hbm.1, f32[1,32,128,128]{3,2,1,0:T(8,128)} %a_hbm.1, f32[1,128,128]{2,1,0:T(8,128)} %e_hbm.1, f32[1,8,128,128]{3,2,1,0:T(8,128)} %b_hbm.1), custom_call_target="tpu_custom_call" | custom-call | tf_op jit(solution)/shard_map/pallas_call | solution.py:305
  70.6 3.1 %copy.8 = f32[1024,512]{1,0:T(8,128)} copy(f32[1024,512]{1,0:T(8,128)} %shard_map.64) | data formatting | bytes 4194304

commit v2 on v1

v2 whole, which is shorter than its diff:
```python
import jax
import jax.numpy as jnp
from jax import lax
from jax.experimental import pallas as pl
from jax.experimental.pallas import tpu as pltpu
from jax.sharding import PartitionSpec as P

MESH = pl.DeviceIdType.MESH
F32, BF16 = jnp.float32, jnp.bfloat16
NY, NZ, NC = 4, 8, 8
LEAF, R, PC = 1024, 128, 512
HALF = PC // 2
NN = (((1,), (0,)), ((), ()))
NT = (((1,), (1,)), ((), ()))


def split(v):
    hi = v.astype(BF16)
    return hi, (v - hi.astype(F32)).astype(BF16)


def dot3(a, b, dims):
    (ah, al), (bh, bl) = a, b

    def one(u, v):
        return lax.dot_general(u, v, dims, preferred_element_type=F32)

    return one(ah, bh) + one(ah, bl) + one(al, bh)


GROUPS = ((4,), (3, 5), (2, 6), (1, 7))
QUARTERS, QROWS = 4, PC // 4
PIECE = R // NZ
ORDER = {1: (0, 1, 2, 3), -1: (2, 3, 0, 1)}


def steps(sign, quarter, size):
    return size // 2 if quarter in ORDER[sign][:2] else size // 2 - 1


def kernel(
    x_hbm, d_hbm, u_hbm, a_hbm, e_hbm, b_hbm, near_out, tot_out,
    near, tot, av, xv, dv, uv, xh, xl, a2, ah, al, cc, cr, crh, crl, er, bv, p2, rz, p1, ry, gs, gz, gp, gx, ts, tx, hp, hz, hy,
    lsem, ssem, rsem,
):
    leaf = lax.axis_index("leaf")
    clu = lax.axis_index("cluster")
    y, z = leaf // NZ, lax.rem(leaf, NZ)
    counts = {"local": 0, "remote": 0}
    started = []

    def at_y(d):
        return {"leaf": lax.rem(y + d + NY, NY) * NZ + z}

    def at_z(d):
        return {"leaf": y * NZ + lax.rem(z + d + NZ, NZ)}

    def at_c(d):
        return {"cluster": lax.rem(clu + d + NC, NC)}

    barrier = pltpu.get_barrier_semaphore()
    partners = [at_y(d) for d in range(1, NY)] + [at_z(d) for d in range(1, NZ)] + [at_c(d) for d in range(1, NC)]
    for partner in partners:
        pl.semaphore_signal(barrier, inc=1, device_id=partner, device_id_type=MESH)

    def load(src, dst):
        i = counts["local"]
        counts["local"] += 1
        copy = pltpu.make_async_copy(src, dst, lsem.at[i])
        copy.start()
        return copy

    def send(src, dst, where):
        i = counts["remote"]
        counts["remote"] += 1
        copy = pltpu.make_async_remote_copy(
            src_ref=src, dst_ref=dst, send_sem=ssem.at[i], recv_sem=rsem.at[i], device_id=where, device_id_type=MESH
        )
        copy.start()
        started.append(copy)
        return copy

    load_x = load(x_hbm, xv)
    load_u = load(u_hbm, uv)
    load_d = load(d_hbm, dv)
    load_e = load(e_hbm.at[0], er.at[0])
    load_a = load(a_hbm.at[0], av)
    own_a = {d: load(a_hbm.at[0, y * NZ + lax.rem(z + d, NZ)], a2.at[0, d]) for d in range(1, NZ)}
    own_y = [load(a_hbm.at[0, lax.rem(y + d, NY) * NZ + z], a2.at[d, 0]) for d in range(1, NY)]
    load_b = [load(b_hbm.at[0, lax.rem(clu - d + NC, NC)], bv.at[d]) for d in range(1, NC)]

    load_x.wait()
    load_u.wait()
    h, l = split(xv[...])
    xh[...] = h
    xl[...] = l
    coef = dot3(split(uv[...].T), (xh[...], xl[...]), NN).T
    cc[0] = coef
    cr[0] = coef

    pl.semaphore_wait(barrier, len(partners))

    def rows(quarter):
        return pl.ds(quarter * QROWS, QROWS)

    moves = {}

    def gather_step(ref, size, where, sign, quarter, step):
        def slot(n):
            return (-sign * n) % size

        moves[size, sign, quarter, step] = send(
            ref.at[slot(step - 1), rows(quarter)], ref.at[slot(step), rows(quarter)], where(sign)
        )

    def gather_event(ref, size, where, k):
        step, place = k // QUARTERS + 1, k % QUARTERS
        for sign in (1, -1):
            quarter = ORDER[sign][place]
            if step <= steps(sign, quarter, size):
                moves[size, sign, quarter, step].wait_recv()
                if step < steps(sign, quarter, size):
                    gather_step(ref, size, where, sign, quarter, step + 1)

    def z_event(k):
        gather_event(cc, NZ, at_z, k)

    def y_event(k):
        gather_event(cr, NY, at_y, k)

    for place in range(QUARTERS):
        for sign in (1, -1):
            gather_step(cc, NZ, at_z, sign, ORDER[sign][place], 1)
        for sign in (1, -1):
            gather_step(cr, NY, at_y, sign, ORDER[sign][place], 1)

    cores = {}

    def send_cores(group):
        for d in group:
            for dy in (2, 1, 3):
                target = lax.rem(y + dy, NY) * NZ + lax.rem(z + d, NZ)
                cores[d, dy] = send(av.at[target], a2.at[NY - dy, d], at_y(dy))

    writes = []

    def near_chunk(i):
        size = LEAF // 4
        part = slice(i * size, (i + 1) * size)
        sym = dv[part, :] + dv[:, part].T
        near[part, :] = dot3(split(sym), (xh[...], xl[...]), NN)
        writes.append(load(near.at[part], near_out.at[part]))

    def send_maps():
        return [send(er.at[0], er.at[NY - dy], at_y(dy)) for dy in (1, 3, 2)]

    load_e.wait()
    maps_y = send_maps()
    load_d.wait()
    near_chunk(0)
    near_chunk(1)
    z_event(0)
    y_event(0)
    z_event(1)
    y_event(1)
    load_a.wait()
    send_cores(GROUPS[0])
    z_event(2)
    near_chunk(2)
    z_event(3)
    near_chunk(3)
    z_event(4)
    for copy in own_y:
        copy.wait()
    own_h, own_l = split(jnp.concatenate([a2[d, 0] for d in range(1, NY)], axis=1))
    h, l = split(cr[0])
    crh[:, :R] = h
    crl[:, :R] = l
    t = dot3((crh[:, :R], crl[:, :R]), (own_h, own_l), NN)
    for d in range(1, NY):
        p1[d] = t[:, (d - 1) * R : d * R]
    z_event(5)
    y_event(2)
    y_event(3)
    send_cores(GROUPS[1])
    z_event(6)
    y_event(4)
    y_event(5)
    send_cores(GROUPS[2])
    send_cores(GROUPS[3])

    for r in range(1, NY):
        h, l = split(cr[r])
        crh[:, r * R : (r + 1) * R] = h
        crl[:, r * R : (r + 1) * R] = l
    z_event(7)

    for copy in maps_y:
        copy.wait_recv()
    mine = pl.ds(pl.multiple_of(y * R, R), R)
    g = jnp.zeros((R, R), F32)
    for r in range(NY):
        g = g + dot3(split(cr[r, mine, :]), split(er[r]), NN)
    gs[...] = g

    def piece(at):
        return pl.ds(pl.multiple_of(at * PIECE, PIECE), PIECE)

    g_z = [send(gs.at[piece(lax.rem(z + d, NZ))], gz.at[d], at_z(d)) for d in (4, 3, 5, 2, 6, 1, 7)]
    z_event(8)
    p2[0] = dot3((crh[:, R:], crl[:, R:]), (own_h, own_l), NT)
    z_event(9)

    def second(group):
        for d in group:
            for dy in (2, 1, 3):
                cores[d, dy].wait_recv()
            own_a[d].wait()
            h, l = split(a2[:, d].reshape(NY * R, R))
            ah[d] = h
            al[d] = l
        b = tuple(jnp.concatenate([m[d] for d in group], axis=1) for m in (ah, al))
        t = dot3((crh[...], crl[...]), b, NN)
        for i, d in enumerate(group):
            p2[d] = t[:, i * R : (i + 1) * R]

    sums = {}

    def sum_step(sign, quarter, step):
        length = steps(sign, quarter, NZ)
        at = (sign * (length - step)) % NZ
        way = 0 if sign > 0 else 1
        if step > 0:
            sums[sign, quarter, step].wait_recv()
            p2[at, rows(quarter)] = p2[at, rows(quarter)] + rz[way, quarter, step - 1]
        sums[sign, quarter, step + 1] = send(p2.at[at, rows(quarter)], rz.at[way, quarter, step], at_z(sign))

    def sum_steps(places, step):
        for place in places:
            for sign in (1, -1):
                sum_step(sign, ORDER[sign][place], step)

    def first(group, fresh, part=range(NY)):
        a = split(jnp.concatenate([cc[d] for d in group], axis=1))
        b = tuple(jnp.concatenate([m[d, part[0] * R : (part[-1] + 1) * R] for d in group], axis=1) for m in (ah, al))
        t = dot3(a, b, NT)
        for i, r in enumerate(part):
            new = t[:, i * R : (i + 1) * R]
            p1[r] = new if fresh and r == 0 else p1[r] + new

    second(GROUPS[0])
    sum_steps((0, 1), 0)

    for copy in g_z:
        copy.wait_recv()
    own_piece = gs[piece(z), :]
    for d in range(1, NZ):
        own_piece = own_piece + gz[d]
    gp[...] = own_piece
    g_c = [send(gp, gx.at[d], at_c(d)) for d in range(1, NC)]
    for copy in load_b:
        copy.wait()
    halves = split(own_piece)
    for d in range(1, NC):
        ts[d] = dot3(halves, split(bv[d]), NN)
    t_c = [send(ts.at[d], tx.at[d], at_c(-d)) for d in range(1, NC)]

    second(GROUPS[1])
    sum_steps((2, 3), 0)
    sum_steps((0, 1), 1)

    for copy in g_c + t_c:
        copy.wait_recv()
    field = tx[1]
    for d in range(2, NC):
        field = field + tx[d]
    for d in range(1, NC):
        field = field + dot3(split(gx[d]), split(bv[d]), NT)
    hp[...] = field
    hz[piece(z), :] = field
    h_z = [send(hp, hz.at[piece(z)], at_z(d)) for d in (4, 3, 5, 2, 6, 1, 7)]

    for k in range(10, 14):
        z_event(k)
    first(GROUPS[0], True)

    second(GROUPS[2])
    sum_steps((2, 3), 1)
    sum_steps((0, 1), 2)
    first(GROUPS[1], False)
    first(GROUPS[2], False)

    for copy in h_z:
        copy.wait_recv()
    hy[mine, :] = hz[...]
    h_y = [send(hz, hy.at[mine], at_y(dy)) for dy in (1, 3, 2)]
    second(GROUPS[3])

    sums_y = {}

    def sum_y(sign, quarter, step):
        length = steps(sign, quarter, NY)
        at = (sign * (length - step)) % NY
        way = 0 if sign > 0 else 1
        if step > 0:
            sums_y[sign, quarter, step].wait_recv()
            p1[at, rows(quarter)] = p1[at, rows(quarter)] + ry[way, quarter, step - 1]
        sums_y[sign, quarter, step + 1] = send(p1.at[at, rows(quarter)], ry.at[way, quarter, step], at_y(sign))

    first(GROUPS[3], False, range(2, 4))
    for place in (0, 1):
        for sign in (1, -1):
            sum_y(sign, ORDER[sign][place], 0)
    first(GROUPS[3], False, range(0, 2))
    for place in (2, 3):
        for sign in (1, -1):
            sum_y(sign, ORDER[sign][place], 0)
    sum_steps((2, 3), 2)
    sum_steps((0, 1), 3)
    for place in (0, 1):
        for sign in (1, -1):
            sum_y(sign, ORDER[sign][place], 1)

    for copy in h_y:
        copy.wait_recv()
    total = p1[0] + p2[0] + dot3(split(hy[...]), split(er[0]), NT)
    tot[...] = total
    for place in (2, 3, 0, 1):
        for sign in (1, -1):
            quarter = ORDER[sign][place]
            length = steps(sign, quarter, NZ)
            sums[sign, quarter, length].wait_recv()
            tot[rows(quarter), :] = tot[rows(quarter), :] + rz[0 if sign > 0 else 1, quarter, length - 1]
    for place in (2, 3, 0, 1):
        for sign in (1, -1):
            quarter = ORDER[sign][place]
            length = steps(sign, quarter, NY)
            sums_y[sign, quarter, length].wait_recv()
            tot[rows(quarter), :] = tot[rows(quarter), :] + ry[0 if sign > 0 else 1, quarter, length - 1]
    writes.append(load(tot, tot_out))
    for copy in started:
        copy.wait_send()
    for copy in writes:
        copy.wait()


def last(near, u, tot, out, held, sems):
    total = split(tot[...])
    copies = []
    for i in range(4):
        part = pl.ds(i * (LEAF // 4), LEAF // 4)
        held[part, :] = near[part, :] + dot3(split(u[part, :]), total, NT)
        copies.append(pltpu.make_async_copy(held.at[part], out.at[part], sems.at[i]))
        copies[-1].start()
    for copy in copies:
        copy.wait()


N_LOCAL, N_REMOTE = 32, 144


def local(probes, dense_leaf, leaf_basis, sibling_cores, transfer, cluster_cores):
    arrays = (probes, dense_leaf, leaf_basis, sibling_cores, transfer, cluster_cores)
    hbm = pl.BlockSpec(memory_space=pltpu.HBM)
    vmem = pltpu.VMEM
    scratch = [
        vmem((LEAF, PC), F32), vmem((PC, R), F32), vmem((NY * NZ, R, R), F32), vmem((LEAF, PC), F32), vmem((LEAF, LEAF), F32), vmem((LEAF, R), F32), vmem((LEAF, PC), BF16), vmem((LEAF, PC), BF16),
        vmem((NY, NZ, R, R), F32), vmem((NZ, NY * R, R), BF16), vmem((NZ, NY * R, R), BF16),
        vmem((NZ, PC, R), F32), vmem((NY, PC, R), F32), vmem((PC, NY * R), BF16), vmem((PC, NY * R), BF16),
        vmem((NY, R, R), F32), vmem((NC, R, R), F32),
        vmem((NZ, PC, R), F32), vmem((2, QUARTERS, NZ // 2, QROWS, R), F32), vmem((NY, PC, R), F32),
        vmem((2, QUARTERS, NY // 2, QROWS, R), F32),
        vmem((R, R), F32), vmem((NZ, PIECE, R), F32), vmem((PIECE, R), F32), vmem((NC, PIECE, R), F32),
        vmem((NC, PIECE, R), F32), vmem((NC, PIECE, R), F32), vmem((PIECE, R), F32), vmem((R, R), F32), vmem((PC, R), F32),
        pltpu.SemaphoreType.DMA((N_LOCAL,)), pltpu.SemaphoreType.DMA((N_REMOTE,)), pltpu.SemaphoreType.DMA((N_REMOTE,)),
    ]
    near, total = pl.pallas_call(
        kernel,
        out_shape=(jax.ShapeDtypeStruct((LEAF, PC), F32), jax.ShapeDtypeStruct((PC, R), F32)),
        in_specs=[hbm] * 6,
        out_specs=[pl.BlockSpec(memory_space=pl.ANY)] * 2,
        scratch_shapes=scratch,
        compiler_params=pltpu.CompilerParams(collective_id=0, has_side_effects=True, vmem_limit_bytes=34 * 2**20),
    )(*[pltpu.with_memory_space_constraint(v, pltpu.HBM) for v in arrays])
    return pl.pallas_call(
        last,
        out_shape=jax.ShapeDtypeStruct((LEAF, PC), F32),
        in_specs=[pl.BlockSpec(memory_space=vmem)] * 3,
        out_specs=hbm,
        scratch_shapes=[vmem((LEAF, PC), F32), pltpu.SemaphoreType.DMA((4,))],
        compiler_params=pltpu.CompilerParams(vmem_limit_bytes=16 * 2**20),
    )(near, leaf_basis, total)


def solution(mesh):
    both = P(("cluster", "leaf"), None)
    return jax.shard_map(
        local,
        mesh=mesh,
        in_specs=(
            both, both, both, P(("cluster", "leaf"), None, None, None), P(("cluster", "leaf"), None, None),
            P("cluster", None, None, None),
        ),
        out_specs=both,
        check_vma=False,
    )
```

time: 74.8 us -> 60 us (0.80); the launches traced: 73.7 us -> 60 us
  Pallas kernels: 70.6 us -> 60 us
  local copies, waits for them, and re-layouts: 3.08 us -> 0.01 us
    pallas_call x1 -> x2, Pallas kernels: 70.6 us -> 60 us  [the longest x1 58.1 us: local(): pl.pallas_call(kernel, out_shape=(jax.ShapeDtypeStruct((LEAF, PC), F32),...]
    unnamed x1 -> x2, local copies, waits for them, and re-layouts: 3.08 us -> 0.01 us
where the time goes in v2:
time: 60 us
  Pallas kernels  60 us (100%)
    pallas_call x1, Pallas kernels, local(): pl.pallas_call(kernel, out_shape=(jax.ShapeDtypeStruct((LEAF, PC), F32),...  58.1 us
    pallas_call x1, Pallas kernels, local(): pl.pallas_call(last, out_shape=jax.ShapeDtypeStruct((LEAF, PC), F32), in_...  1.81 us

profile of v2, /device:TPU:4, one launch (start us, length us, event | category | flops | bytes accessed | tf_op | source)
XLA Modules:
  0.0 60.0 jit_solution(6869707732652847253)
XLA Ops:
  0.0 0.0 copy-start
  0.0 58.1 %shard_map.64 = (f32[1024,512]{1,0:T(8,128)S(1)}, f32[512,128]{1,0:T(8,128)S(1)}) custom-call(f32[1024,512]{1,0:T(8,128)} %x_hbm.1, f32[1024,1024]{1,0:T(8,128)} %d_hbm.1, f32[1024,128]{1,0:T(8,128)} %u.1, f32[1,32,128,128]{3,2,1,0:T(8,128)} %a_hbm.1, f32[1,128,128]{2,1,0:T(8,128)} %e_hbm.1, f32[1,8,128,128]{3,2,1,0:T(8,128)} %b_hbm.1), custom_call_target="tpu_custom_call" | custom-call | tf_op jit(solution)/shard_map/pallas_call | solution.py:377
  58.2 0.0 copy-done
  58.2 1.8 %shard_map.65 = f32[1024,512]{1,0:T(8,128)} custom-call(f32[1024,512]{1,0:T(8,128)S(1)} %get-tuple-element.7.near, f32[1024,128]{1,0:T(8,128)S(1)} %copy-done, f32[512,128]{1,0:T(8,128)S(1)} %get-tuple-element.8.tot), custom_call_target="tpu_custom_call" | custom-call | tf_op jit(solution)/shard_map/pallas_call | solution.py:385
Async XLA Ops:
  0.0 58.2 %copy-start = (f32[1024,128]{1,0:T(8,128)S(1)}, f32[1024,128]{1,0:T(8,128)}, u32[]{:S(2)}) copy-start(f32[1024,128]{1,0:T(8,128)} %u.1) | copy-start | bytes 1572868

commit v3 on v2

v3 whole, which is shorter than its diff:
```python
import jax
import jax.numpy as jnp
from jax import lax
from jax.experimental import pallas as pl
from jax.experimental.pallas import tpu as pltpu
from jax.sharding import PartitionSpec as P

MESH = pl.DeviceIdType.MESH
F32, BF16 = jnp.float32, jnp.bfloat16
NY, NZ, NC = 4, 8, 8
LEAF, R, PC = 1024, 128, 512
HALF = PC // 2
NN = (((1,), (0,)), ((), ()))
NT = (((1,), (1,)), ((), ()))


def split(v):
    hi = v.astype(BF16)
    return hi, (v - hi.astype(F32)).astype(BF16)


def dot3(a, b, dims):
    (ah, al), (bh, bl) = a, b

    def one(u, v):
        return lax.dot_general(u, v, dims, preferred_element_type=F32)

    return one(ah, bh) + one(ah, bl) + one(al, bh)


GROUPS = ((4,), (3, 5), (2, 6), (1, 7))
QUARTERS, QROWS = 4, PC // 4
PIECE = R // NZ
ORDER = {1: (0, 1, 2, 3), -1: (2, 3, 0, 1)}


def steps(sign, quarter, size):
    return size // 2 if quarter in ORDER[sign][:2] else size // 2 - 1


def kernel(
    x_hbm, d_hbm, u_hbm, a_hbm, e_hbm, b_hbm, near_out, tot_out,
    near, tot, av, xv, dv, uv, xh, xl, a2, ah, al, cc, cr, crh, crl, er, bv, p2, rz, p1, ry, gs, gz, gp, gx, ts, tx, hp, hz,
    lsem, ssem, rsem,
):
    leaf = lax.axis_index("leaf")
    clu = lax.axis_index("cluster")
    y, z = leaf // NZ, lax.rem(leaf, NZ)
    ids = {}

    def number(kind, key):
        return ids.setdefault((kind, key), sum(k == kind for k, _ in ids))

    def at_y(d):
        return {"leaf": lax.rem(y + d + NY, NY) * NZ + z}

    def at_z(d):
        return {"leaf": y * NZ + lax.rem(z + d + NZ, NZ)}

    def at_c(d):
        return {"cluster": lax.rem(clu + d + NC, NC)}

    barrier = pltpu.get_barrier_semaphore()
    partners = [at_y(d) for d in range(1, NY)] + [at_z(d) for d in range(1, NZ)] + [at_c(d) for d in range(1, NC)]
    for partner in partners:
        pl.semaphore_signal(barrier, inc=1, device_id=partner, device_id_type=MESH)

    def load(src, dst, key):
        copy = pltpu.make_async_copy(src, dst, lsem.at[number("local", key)])
        copy.start()

    def send(src, dst, where, out, key):
        pltpu.make_async_remote_copy(
            src_ref=src, dst_ref=dst, send_sem=ssem.at[number("send", out)], recv_sem=rsem.at[number("recv", key)],
            device_id=where, device_id_type=MESH,
        ).start()

    def wait(kind, ref, key):
        sem = {"local": lsem, "send": ssem, "recv": rsem}[kind].at[ids[kind, key]]
        pltpu.make_async_copy(ref, ref, sem).wait()

    load(u_hbm, uv, "u")
    load(e_hbm.at[0], er.at[0], "e")
    XROWS = LEAF // 4
    for i in range(4):
        part = pl.ds(i * XROWS, XROWS)
        load(x_hbm.at[part], xv.at[part], ("x", i))

    wait("local", uv, "u")
    uh, ul = split(uv[...].T)
    coef = jnp.zeros((R, PC), F32)
    for i in range(4):
        part = slice(i * XROWS, (i + 1) * XROWS)
        wait("local", xv.at[pl.ds(i * XROWS, XROWS)], ("x", i))
        if i == 3:
            load(a_hbm.at[0], av, "a")
            load(d_hbm, dv, "d")
            for d in range(1, NY):
                load(a_hbm.at[0, lax.rem(y + d, NY) * NZ + z], a2.at[d, 0], "own_y")
            for d in range(1, NZ):
                load(a_hbm.at[0, y * NZ + lax.rem(z + d, NZ)], a2.at[0, d], "own_a")
            for d in range(1, NC):
                load(b_hbm.at[0, lax.rem(clu - d + NC, NC)], bv.at[d], "b")
        h, l = split(xv[part, :])
        xh[part, :] = h
        xl[part, :] = l
        coef = coef + dot3((uh[:, part], ul[:, part]), (h, l), NN)
    coef = coef.T
    cc[0] = coef
    cr[0] = coef

    pl.semaphore_wait(barrier, len(partners))

    def rows(quarter):
        return pl.ds(quarter * QROWS, QROWS)

    PAIR = pl.ds(0, 2 * QROWS)

    def gather_step(ref, size, where, sign, place, step):
        def slot(n):
            return (-sign * n) % size

        part = rows(ORDER[sign][place])
        send(ref.at[slot(step - 1), part], ref.at[slot(step), part], where(sign), ("gather", size), ("gather", size, place, step))

    def gather_event(ref, size, where, k):
        step, place = k // QUARTERS + 1, k % QUARTERS
        wait("recv", ref.at[0, PAIR], ("gather", size, place, step))
        for sign in (1, -1):
            if step < steps(sign, ORDER[sign][place], size):
                gather_step(ref, size, where, sign, place, step + 1)

    def z_event(k):
        gather_event(cc, NZ, at_z, k)

    def y_event(k):
        gather_event(cr, NY, at_y, k)

    for place in range(QUARTERS):
        for sign in (1, -1):
            gather_step(cc, NZ, at_z, sign, place, 1)
        for sign in (1, -1):
            gather_step(cr, NY, at_y, sign, place, 1)

    def send_cores(group):
        for d in group:
            for dy in (2, 1, 3):
                target = lax.rem(y + dy, NY) * NZ + lax.rem(z + d, NZ)
                send(av.at[target], a2.at[NY - dy, d], at_y(dy), "cores", ("cores", d))

    def near_chunk(i):
        size = LEAF // 4
        part = slice(i * size, (i + 1) * size)
        sym = dv[part, :] + dv[:, part].T
        near[part, :] = dot3(split(sym), (xh[...], xl[...]), NN)
        load(near.at[part], near_out.at[part], "near")

    wait("local", er.at[0], "e")
    for dy in (1, 3, 2):
        send(er.at[0], er.at[NY - dy], at_y(dy), "maps", "maps")
    z_event(0)
    y_event(0)
    z_event(1)
    y_event(1)
    wait("local", av, "a")
    send_cores(GROUPS[0])
    z_event(2)
    z_event(3)
    wait("local", dv, "d")
    near_chunk(0)
    z_event(4)
    y_event(2)
    y_event(3)
    send_cores(GROUPS[1])
    z_event(5)
    y_event(4)
    y_event(5)
    send_cores(GROUPS[2])
    send_cores(GROUPS[3])
    z_event(6)

    for r in range(NY):
        h, l = split(cr[r])
        crh[:, r * R : (r + 1) * R] = h
        crl[:, r * R : (r + 1) * R] = l
    z_event(7)

    wait("recv", er.at[pl.ds(1, NY - 1)], "maps")
    mine = pl.ds(pl.multiple_of(y * R, R), R)
    g = jnp.zeros((R, R), F32)
    for r in range(NY):
        g = g + dot3(split(cr[r, mine, :]), split(er[r]), NN)
    gs[...] = g

    def piece(at):
        return pl.ds(pl.multiple_of(at * PIECE, PIECE), PIECE)

    for d in (4, 3, 5, 2, 6, 1, 7):
        send(gs.at[piece(lax.rem(z + d, NZ))], gz.at[d], at_z(d), "gz", "gz")
    z_event(8)
    z_event(9)

    wait("local", a2.at[0, pl.ds(1, NZ - 1)], "own_a")

    def second(group):
        for d in group:
            wait("recv", a2.at[pl.ds(1, NY - 1), d], ("cores", d))
            h, l = split(a2[:, d].reshape(NY * R, R))
            ah[d] = h
            al[d] = l
        b = tuple(jnp.concatenate([m[d] for d in group], axis=1) for m in (ah, al))
        t = dot3((crh[...], crl[...]), b, NN)
        for i, d in enumerate(group):
            p2[d] = t[:, i * R : (i + 1) * R]

    def sum_step(ref, got, size, where, place, step):
        if step > 0:
            wait("recv", ref.at[0, PAIR], ("sum", size, place, step - 1))
        for way, sign in enumerate((1, -1)):
            quarter = ORDER[sign][place]
            at = (sign * (steps(sign, quarter, size) - step)) % size
            part = rows(quarter)
            if step > 0:
                ref[at, part] = ref[at, part] + got[way, quarter, step - 1]
            send(ref.at[at, part], got.at[way, quarter, step], where(sign), ("sum", size), ("sum", size, place, step))

    def sum_last(ref, got, size, place):
        for way, sign in enumerate((1, -1)):
            quarter = ORDER[sign][place]
            length = steps(sign, quarter, size)
            if way == 0:
                wait("recv", ref.at[0, PAIR], ("sum", size, place, length - 1))
            tot[rows(quarter), :] = tot[rows(quarter), :] + got[way, quarter, length - 1]

    def sum_steps(places, step):
        for place in places:
            sum_step(p2, rz, NZ, at_z, place, step)

    def first(group, fresh, part=range(NY)):
        a = split(jnp.concatenate([cc[d] for d in group], axis=1))
        b = tuple(jnp.concatenate([m[d, part[0] * R : (part[-1] + 1) * R] for d in group], axis=1) for m in (ah, al))
        t = dot3(a, b, NT)
        for i, r in enumerate(part):
            new = t[:, i * R : (i + 1) * R]
            p1[r] = new if fresh and r == 0 else p1[r] + new

    second(GROUPS[0])
    sum_steps((0, 1), 0)
    near_chunk(1)

    wait("local", a2.at[pl.ds(1, NY - 1), 0], "own_y")
    own = split(jnp.concatenate([a2[d, 0] for d in range(1, NY)], axis=1))
    t = dot3((crh[:, :R], crl[:, :R]), own, NN)
    for d in range(1, NY):
        p1[d] = t[:, (d - 1) * R : d * R]
    p2[0] = dot3((crh[:, R:], crl[:, R:]), own, NT)

    wait("recv", gz.at[pl.ds(1, NZ - 1)], "gz")
    own_piece = gs[piece(z), :]
    for d in range(1, NZ):
        own_piece = own_piece + gz[d]
    gp[...] = own_piece
    for d in range(1, NC):
        send(gp, gx.at[d], at_c(d), "gx", "gx")
    wait("local", bv.at[pl.ds(1, NC - 1)], "b")
    halves = split(own_piece)
    for d in range(1, NC):
        ts[d] = dot3(halves, split(bv[d]), NN)
    for d in range(1, NC):
        send(ts.at[d], tx.at[d], at_c(-d), "tx", "tx")

    second(GROUPS[1])
    sum_steps((2, 3), 0)
    for k in range(10, 14):
        z_event(k)
    first(GROUPS[0], True)
    sum_steps((0, 1), 1)

    wait("recv", gx.at[pl.ds(1, NC - 1)], "gx")
    wait("recv", tx.at[pl.ds(1, NC - 1)], "tx")
    field = tx[1]
    for d in range(2, NC):
        field = field + tx[d]
    for d in range(1, NC):
        field = field + dot3(split(gx[d]), split(bv[d]), NT)
    hp[...] = field
    hz[piece(z), :] = field
    for d in (4, 3, 5, 2, 6, 1, 7):
        send(hp, hz.at[piece(z)], at_z(d), "hz", "hz")

    first(GROUPS[1], False)
    second(GROUPS[2])
    sum_steps((2, 3), 1)
    near_chunk(2)
    sum_steps((0, 1), 2)
    first(GROUPS[2], False)

    wait("recv", hz.at[pl.ds(0, R - PIECE)], "hz")
    t = dot3(split(hz[...]), split(er[...].reshape(NY * R, R)), NT)
    for r in range(NY):
        p1[r, mine, :] = p1[r, mine, :] + t[:, r * R : (r + 1) * R]
    second(GROUPS[3])

    first(GROUPS[3], False, range(2, 4))
    for place in (0, 1):
        sum_step(p1, ry, NY, at_y, place, 0)
    first(GROUPS[3], False, range(0, 2))
    for place in (2, 3):
        sum_step(p1, ry, NY, at_y, place, 0)
    sum_steps((2, 3), 2)
    near_chunk(3)
    for place in (0, 1):
        sum_step(p2, rz, NZ, at_z, place, 3)
        sum_step(p1, ry, NY, at_y, place, 1)

    tot[...] = p1[0] + p2[0]
    for place in (2, 3, 0, 1):
        sum_last(p2, rz, NZ, place)
    for place in (2, 3, 0, 1):
        sum_last(p1, ry, NY, place)
    load(tot, tot_out, "tot")
    for size, ref in ((NZ, cc), (NY, cr)):
        for what in ("gather", "sum"):
            wait("send", ref.at[pl.ds(1, size - 1)], (what, size))
    wait("send", a2.at[pl.ds(1, NY - 1), pl.ds(1, NZ - 1)], "cores")
    wait("send", er.at[pl.ds(1, NY - 1)], "maps")
    wait("send", gz.at[pl.ds(1, NZ - 1)], "gz")
    wait("send", gx.at[pl.ds(1, NC - 1)], "gx")
    wait("send", tx.at[pl.ds(1, NC - 1)], "tx")
    wait("send", hz.at[pl.ds(0, R - PIECE)], "hz")
    wait("local", near, "near")
    wait("local", tot, "tot")


def last(near, u, tot, out, held, sems):
    high, low = split(tot[...])
    twice = jnp.concatenate([high, high], axis=1)
    copies = []
    for i in range(4):
        part = pl.ds(i * (LEAF // 4), LEAF // 4)
        h, l = split(u[part, :])
        far = lax.dot_general(jnp.concatenate([h, l], axis=1), twice, NT, preferred_element_type=F32)
        held[part, :] = near[part, :] + (far + lax.dot_general(h, low, NT, preferred_element_type=F32))
        copies.append(pltpu.make_async_copy(held.at[part], out.at[part], sems.at[i]))
        copies[-1].start()
    for copy in copies:
        copy.wait()


N_LOCAL, N_SEND, N_RECV = 13, 10, 52


def local(probes, dense_leaf, leaf_basis, sibling_cores, transfer, cluster_cores):
    arrays = (probes, dense_leaf, leaf_basis, sibling_cores, transfer, cluster_cores)
    hbm = pl.BlockSpec(memory_space=pltpu.HBM)
    vmem = pltpu.VMEM
    scratch = [
        vmem((LEAF, PC), F32), vmem((PC, R), F32), vmem((NY * NZ, R, R), F32), vmem((LEAF, PC), F32), vmem((LEAF, LEAF), F32), vmem((LEAF, R), F32), vmem((LEAF, PC), BF16), vmem((LEAF, PC), BF16),
        vmem((NY, NZ, R, R), F32), vmem((NZ, NY * R, R), BF16), vmem((NZ, NY * R, R), BF16),
        vmem((NZ, PC, R), F32), vmem((NY, PC, R), F32), vmem((PC, NY * R), BF16), vmem((PC, NY * R), BF16),
        vmem((NY, R, R), F32), vmem((NC, R, R), F32),
        vmem((NZ, PC, R), F32), vmem((2, QUARTERS, NZ // 2, QROWS, R), F32), vmem((NY, PC, R), F32),
        vmem((2, QUARTERS, NY // 2, QROWS, R), F32),
        vmem((R, R), F32), vmem((NZ, PIECE, R), F32), vmem((PIECE, R), F32), vmem((NC, PIECE, R), F32),
        vmem((NC, PIECE, R), F32), vmem((NC, PIECE, R), F32), vmem((PIECE, R), F32), vmem((R, R), F32),
        pltpu.SemaphoreType.DMA((N_LOCAL,)), pltpu.SemaphoreType.DMA((N_SEND,)), pltpu.SemaphoreType.DMA((N_RECV,)),
    ]
    near, total = pl.pallas_call(
        kernel,
        out_shape=(jax.ShapeDtypeStruct((LEAF, PC), F32), jax.ShapeDtypeStruct((PC, R), F32)),
        in_specs=[hbm] * 6,
        out_specs=[pl.BlockSpec(memory_space=pl.ANY)] * 2,
        scratch_shapes=scratch,
        compiler_params=pltpu.CompilerParams(collective_id=0, has_side_effects=True, vmem_limit_bytes=34 * 2**20),
    )(*[pltpu.with_memory_space_constraint(v, pltpu.HBM) for v in arrays])
    return pl.pallas_call(
        last,
        out_shape=jax.ShapeDtypeStruct((LEAF, PC), F32),
        in_specs=[pl.BlockSpec(memory_space=vmem)] * 3,
        out_specs=hbm,
        scratch_shapes=[vmem((LEAF, PC), F32), pltpu.SemaphoreType.DMA((4,))],
        compiler_params=pltpu.CompilerParams(vmem_limit_bytes=16 * 2**20),
    )(near, leaf_basis, total)


def solution(mesh):
    both = P(("cluster", "leaf"), None)
    return jax.shard_map(
        local,
        mesh=mesh,
        in_specs=(
            both, both, both, P(("cluster", "leaf"), None, None, None), P(("cluster", "leaf"), None, None),
            P("cluster", None, None, None),
        ),
        out_specs=both,
        check_vma=False,
    )
```

time: 60 us -> 56.5 us (0.942)
  Pallas kernels: 60 us -> 56.2 us
    pallas_call x1, Pallas kernels: 58.1 us -> 54.6 us  [local(): pl.pallas_call(kernel, out_shape=(jax.ShapeDtypeStruct((LEAF, PC), F32),...]
where the time goes in v3:
time: 56.5 us; the launch traced here: 56.4 us
  Pallas kernels  56.2 us (99%)
    pallas_call x1, Pallas kernels, local(): pl.pallas_call(kernel, out_shape=(jax.ShapeDtypeStruct((LEAF, PC), F32),...  54.6 us
    pallas_call x1, Pallas kernels, local(): pl.pallas_call(last, out_shape=jax.ShapeDtypeStruct((LEAF, PC), F32), in_...  1.65 us

profile of v3, /device:TPU:4, one launch (start us, length us, event | category | flops | bytes accessed | tf_op | source)
XLA Modules:
  0.0 56.4 jit_solution(3089826955907030347)
XLA Ops:
  0.0 0.0 copy-start
  0.0 54.6 %shard_map.64 = (f32[1024,512]{1,0:T(8,128)S(1)}, f32[512,128]{1,0:T(8,128)S(1)}) custom-call(f32[1024,512]{1,0:T(8,128)} %x_hbm.1, f32[1024,1024]{1,0:T(8,128)} %d_hbm.1, f32[1024,128]{1,0:T(8,128)} %u.1, f32[1,32,128,128]{3,2,1,0:T(8,128)} %a_hbm.1, f32[1,128,128]{2,1,0:T(8,128)} %e_hbm.1, f32[1,8,128,128]{3,2,1,0:T(8,128)} %b_hbm.1), custom_call_target="tpu_custom_call" | custom-call | tf_op jit(solution)/shard_map/pallas_call | solution.py:368
  54.6 0.0 copy-done
  54.6 1.7 %shard_map.65 = f32[1024,512]{1,0:T(8,128)} custom-call(f32[1024,512]{1,0:T(8,128)S(1)} %get-tuple-element.7.near, f32[1024,128]{1,0:T(8,128)S(1)} %copy-done, f32[512,128]{1,0:T(8,128)S(1)} %get-tuple-element.8.tot), custom_call_target="tpu_custom_call" | custom-call | tf_op jit(solution)/shard_map/pallas_call | solution.py:376
Async XLA Ops:
  0.0 54.6 %copy-start = (f32[1024,128]{1,0:T(8,128)S(1)}, f32[1024,128]{1,0:T(8,128)}, u32[]{:S(2)}) copy-start(f32[1024,128]{1,0:T(8,128)} %u.1) | copy-start | bytes 1572868

commit v4 on v3

--- a/solution.py
+++ b/solution.py
@@ -61,7 +61,7 @@
         return {"cluster": lax.rem(clu + d + NC, NC)}
 
     barrier = pltpu.get_barrier_semaphore()
-    partners = [at_y(d) for d in range(1, NY)] + [at_z(d) for d in range(1, NZ)] + [at_c(d) for d in range(1, NC)]
+    partners = [at_z(d) for d in (1, 7, 2, 6, 3, 5, 4)] + [at_y(d) for d in range(1, NY)] + [at_c(d) for d in range(1, NC)]
     for partner in partners:
         pl.semaphore_signal(barrier, inc=1, device_id=partner, device_id_type=MESH)
 

time: 56.5 us -> 56.5 us (level)
  no operation moved by 1% of the time
where the time goes in v4:
time: 56.5 us; the launch traced here: 56.4 us
  Pallas kernels  56.2 us (99%)
    pallas_call x1, Pallas kernels, local(): pl.pallas_call(kernel, out_shape=(jax.ShapeDtypeStruct((LEAF, PC), F32),...  54.6 us
    pallas_call x1, Pallas kernels, local(): pl.pallas_call(last, out_shape=jax.ShapeDtypeStruct((LEAF, PC), F32), in_...  1.65 us

profile of v4, /device:TPU:4, one launch (start us, length us, event | category | flops | bytes accessed | tf_op | source)
XLA Modules:
  0.0 56.4 jit_solution(13736863734551683154)
XLA Ops:
  0.0 0.0 copy-start
  0.0 54.6 %shard_map.64 = (f32[1024,512]{1,0:T(8,128)S(1)}, f32[512,128]{1,0:T(8,128)S(1)}) custom-call(f32[1024,512]{1,0:T(8,128)} %x_hbm.1, f32[1024,1024]{1,0:T(8,128)} %d_hbm.1, f32[1024,128]{1,0:T(8,128)} %u.1, f32[1,32,128,128]{3,2,1,0:T(8,128)} %a_hbm.1, f32[1,128,128]{2,1,0:T(8,128)} %e_hbm.1, f32[1,8,128,128]{3,2,1,0:T(8,128)} %b_hbm.1), custom_call_target="tpu_custom_call" | custom-call | tf_op jit(solution)/shard_map/pallas_call | solution.py:368
  54.6 0.0 copy-done
  54.6 1.7 %shard_map.65 = f32[1024,512]{1,0:T(8,128)} custom-call(f32[1024,512]{1,0:T(8,128)S(1)} %get-tuple-element.7.near, f32[1024,128]{1,0:T(8,128)S(1)} %copy-done, f32[512,128]{1,0:T(8,128)S(1)} %get-tuple-element.8.tot), custom_call_target="tpu_custom_call" | custom-call | tf_op jit(solution)/shard_map/pallas_call | solution.py:376
Async XLA Ops:
  0.0 54.6 %copy-start = (f32[1024,128]{1,0:T(8,128)S(1)}, f32[1024,128]{1,0:T(8,128)}, u32[]{:S(2)}) copy-start(f32[1024,128]{1,0:T(8,128)} %u.1) | copy-start | bytes 1572868
